TPU v7x, 128 devices: a whole 4x4x4 slice. The times are simulated.
128 devices in a mesh: dp: 8 (over x, core), pipe: 4 (over y), tensor: 4 (over z).
Axes of the slice: x: 4, y: 4, z: 4, core: 2. Of those that a mesh axis runs over, the one named last changes fastest.
Arguments:
- support_tokens: int32 [64, 32], P(('dp', 'pipe')), may hold values from 0 to 64127
- support_lengths: int32 [64], P(('dp', 'pipe')), may hold values from 1 to 32
- support_labels: int32 [64, 1], P(('dp', 'pipe')), may hold values from 0 to 31
- query_tokens: int32 [32, 32], P(('dp', 'pipe')), may hold values from 0 to 64127
- query_lengths: int32 [32], P(('dp', 'pipe')), may hold values from 1 to 32
- query_episodes: int32 [32], P(('dp', 'pipe')), may hold values from 0 to 1
- embedding: bfloat16 [64128, 4096], P(('dp', 'pipe'), 'tensor'), may hold values from -18 to 18
- attn_gain: float32 [4, 4096], P('pipe'), may hold values from 0.5 to 1.5
- query_weight: bfloat16 [4, 4096, 4096], P('pipe', None, 'tensor'), may hold values from -1 to 1
- key_weight: bfloat16 [4, 4096, 1024], P('pipe', None, 'tensor'), may hold values from -16 to 16
- value_weight: bfloat16 [4, 4096, 1024], P('pipe', None, 'tensor'), may hold values from -0.09375 to 0.09375
- out_weight: bfloat16 [4, 4096, 4096], P('pipe', 'tensor'), may hold values from -0.09375 to 0.09375
- final_gain: float32 [4096], replicated, may hold values from 0.5 to 1.5
Outputs:
- prototypes: float32 [32, 4096], P(None, 'tensor')
- logits: float32 [32, 16], P(('dp', 'pipe'))
Inputs may be any that keep to these rules, and one draw needn't show every extreme that they name: `support_labels`: every class is the label of at least one support sequence.
All inputs are finite; a program needn't handle non-finite values.
Results may differ from a plain program's by a relative error of at most 0.024.
Values may be sent and summed in bfloat16 or wider, within the bound.
A program may use at most 128 MiB of HBM per device.

v0:
```python
import math
import jax
import jax.numpy as jnp
from jax import lax
from jax.sharding import PartitionSpec as P

D = 4096
HEAD_DIM = 128
WAYS = 16
EPISODES = 2
epsilon = 1e-05
rotary_base = 500000.0


def in_order(blocks, dim):
    blocks = jnp.moveaxis(blocks, 0, dim)
    dims = blocks.shape
    return blocks.reshape(*dims[:dim], dims[dim] * dims[dim + 1], *dims[dim + 2 :])


def sent_to_all(shard, axis):
    copies = jnp.broadcast_to(shard, (lax.axis_size(axis), *shard.shape))
    return lax.all_to_all(copies, axis, split_axis=0, concat_axis=0, tiled=True)


def collect(shard, axis, dim):
    return in_order(sent_to_all(shard, axis), dim)


def split_up(shard, dim, length):
    dims = shard.shape
    blocks = shard.reshape(*dims[:dim], length, dims[dim] // length, *dims[dim + 1 :])
    return jnp.moveaxis(blocks, dim, 0)


def sum_at_owner(shard, axis, dim):
    length = lax.axis_size(axis)
    blocks = lax.all_to_all(split_up(shard, dim, length), axis, 0, 0, tiled=True)
    return jnp.sum(blocks.astype(jnp.float32), axis=0)


def passed_along(block, axis, distance):
    devices = range(lax.axis_size(axis))
    route = [((i - distance) % len(devices), i) for i in devices]
    return lax.ppermute(block, axis, route)


def over_copies(shard, axis):
    return sent_to_all(shard, axis).astype(jnp.float32).sum(axis=0)


def rotate(heads_in, seq_len):
    half_dim = HEAD_DIM // 2
    freqs = jnp.exp(
        -math.log(rotary_base) * jnp.arange(half_dim, dtype=jnp.float32) * (2.0 / HEAD_DIM)
    )
    angles = jnp.arange(seq_len, dtype=jnp.float32)[:, None] * freqs[None, :]
    cosine = jnp.cos(angles)[None, :, None, :]
    sine = jnp.sin(angles)[None, :, None, :]
    first_half = heads_in[..., :half_dim]
    second_half = heads_in[..., half_dim:]
    return jnp.concatenate(
        [first_half * cosine - second_half * sine, second_half * cosine + first_half * sine],
        axis=-1,
    )


def whole_rows(hidden):
    return collect(hidden, "tensor", 1)


def whole_values(full_rows, gain_vector):
    values = full_rows.astype(jnp.float32)
    mean_square = jnp.mean(values * values, axis=-1, keepdims=True)
    return values * lax.rsqrt(mean_square + epsilon) * gain_vector


def shards(
    support_tokens,
    support_lengths,
    support_labels,
    query_tokens,
    query_lengths,
    query_episodes,
    embedding,
    attn_gain,
    query_weight,
    key_weight,
    value_weight,
    out_weight,
    final_gain,
):
    group_count = lax.axis_size(("dp", "pipe"))
    sections = lax.axis_size("pipe")
    sup_dev, seq_len = support_tokens.shape
    qry_dev = query_tokens.shape[0]
    seq_count = sup_dev + qry_dev
    row_count = seq_count * seq_len
    table_rows, width = embedding.shape
    column_start = lax.axis_index("tensor") * width
    all_support, all_query, every_sup_len, every_qry_len = (
        lax.all_gather(support_tokens, ("dp", "pipe"), axis=0, tiled=True),
        lax.all_gather(query_tokens, ("dp", "pipe"), axis=0, tiled=True),
        lax.all_gather(support_lengths, ("dp", "pipe"), axis=0, tiled=True),
        lax.all_gather(query_lengths, ("dp", "pipe"), axis=0, tiled=True),
    )
    token_flat = jnp.concatenate(
        [all_support.reshape(group_count, sup_dev * seq_len), all_query], axis=1
    ).reshape(group_count * row_count)
    local_ids = token_flat - lax.axis_index(("dp", "pipe")) * table_rows
    inside = (local_ids >= 0) & (local_ids < table_rows)
    picked = jnp.take(embedding, jnp.clip(local_ids, 0, table_rows - 1), axis=0)
    picked = jnp.where(inside[:, None], picked, jnp.zeros_like(picked))
    replies = lax.all_to_all(picked, ("dp", "pipe"), split_axis=0, concat_axis=0, tiled=True)
    hidden = jnp.sum(
        replies.reshape(group_count, row_count, width).astype(jnp.float32), axis=0
    ).astype(jnp.bfloat16)
    seq_lengths = jnp.concatenate([support_lengths, query_lengths], axis=0)
    query_proj = query_weight[0]
    key_proj = key_weight[0]
    value_proj = value_weight[0]
    out_proj = out_weight[0]
    gain_vector = attn_gain[0]
    local_heads = query_proj.shape[1] // HEAD_DIM
    local_groups = key_proj.shape[1] // HEAD_DIM
    group_size = local_heads // local_groups
    w_in = jnp.concatenate([query_proj, key_proj, value_proj], axis=1)
    query_cols = local_heads * HEAD_DIM
    key_cols = local_groups * HEAD_DIM
    positions = jnp.arange(seq_len)
    causal = positions[None, :] <= positions[:, None]

    def section_block(stream, lengths_here):
        normed = whole_values(whole_rows(stream), gain_vector).astype(jnp.bfloat16)
        projected = jnp.dot(normed, w_in, preferred_element_type=jnp.float32)
        query_heads = projected[:, :query_cols].reshape(seq_count, seq_len, local_heads, HEAD_DIM)
        key_heads = projected[:, query_cols : query_cols + key_cols].reshape(
            seq_count, seq_len, local_groups, HEAD_DIM
        )
        value_heads = (
            projected[:, query_cols + key_cols :]
            .reshape(seq_count, seq_len, local_groups, HEAD_DIM)
            .astype(jnp.bfloat16)
        )
        query_heads = (
            rotate(query_heads, seq_len)
            .astype(jnp.bfloat16)
            .reshape(seq_count, seq_len, local_groups, group_size, HEAD_DIM)
        )
        key_heads = rotate(key_heads, seq_len).astype(jnp.bfloat16)
        scores = jnp.einsum(
            "sikgd,sjkd->skgij", query_heads, key_heads, preferred_element_type=jnp.float32
        ) / math.sqrt(HEAD_DIM)
        visible = causal[None, :, :] & (positions[None, None, :] < lengths_here[:, None, None])
        scores = jnp.where(visible[:, None, None, :, :], scores, -1e30)
        weights = jax.nn.softmax(scores, axis=-1).astype(jnp.bfloat16)
        mixed = jnp.einsum(
            "skgij,sjkd->sikgd", weights, value_heads, preferred_element_type=jnp.float32
        )
        mixed = mixed.astype(jnp.bfloat16).reshape(row_count, query_cols)
        partial_out = jnp.dot(mixed, out_proj, preferred_element_type=jnp.float32)
        summed = sum_at_owner(partial_out.astype(jnp.bfloat16), "tensor", 1)
        return (stream.astype(jnp.float32) + summed).astype(jnp.bfloat16)

    section_index = lax.axis_index("pipe")
    dp_base = lax.axis_index("dp") * sections

    def tick(tick_index, stream):
        held_group = dp_base + (section_index - tick_index) % sections
        sup_part = lax.dynamic_slice_in_dim(every_sup_len, held_group * sup_dev, sup_dev)
        qry_part = lax.dynamic_slice_in_dim(every_qry_len, held_group * qry_dev, qry_dev)
        lengths_here = jnp.concatenate([sup_part, qry_part], axis=0)
        first_tick = (tick_index - section_index) % sections
        active = (first_tick <= tick_index) & (tick_index < first_tick + sections)
        computed = section_block(stream, lengths_here)
        stream = jnp.where(active, computed, stream)
        return passed_along(stream, "pipe", 1)

    hidden = lax.fori_loop(0, 2 * sections, tick, hidden)
    final = lax.dynamic_slice_in_dim(
        whole_values(whole_rows(hidden), final_gain), column_start, width, 1
    )
    live = (positions[None, :] < seq_lengths[:, None]).astype(jnp.float32)
    pooled = jnp.sum(
        final.reshape(seq_count, seq_len, width) * live[:, :, None], axis=1
    ) / seq_lengths[:, None].astype(jnp.float32)
    support_pooled = pooled[:sup_dev]
    query_pooled = pooled[sup_dev:]
    class_count_all = EPISODES * WAYS
    onehot = (support_labels[:, 0][:, None] == jnp.arange(class_count_all)[None, :]).astype(
        jnp.float32
    )
    class_total = jnp.dot(onehot.T, support_pooled, precision=lax.Precision.HIGHEST)
    class_count = jnp.sum(onehot, axis=0)
    class_total, class_count = (
        over_copies(class_total.astype(jnp.bfloat16), ("dp", "pipe")).astype(jnp.float32),
        over_copies(class_count.astype(jnp.bfloat16), ("dp", "pipe")).astype(jnp.float32),
    )
    prototypes = class_total / class_count[:, None]
    episode_pick = (query_episodes[:, None] == jnp.arange(EPISODES)[None, :]).astype(jnp.float32)
    chosen = jnp.einsum(
        "qe,ewc->qwc",
        episode_pick,
        prototypes.reshape(EPISODES, WAYS, width),
        precision=lax.Precision.HIGHEST,
    )
    partial_distance = jnp.sum((query_pooled[:, None, :] - chosen) ** 2, axis=-1)
    distance = lax.psum(partial_distance, "tensor")
    logits = -distance / math.sqrt(D)
    return (prototypes, logits)


def solution(mesh):
    return jax.shard_map(
        shards,
        mesh=mesh,
        in_specs=(
            P(("dp", "pipe"), None),
            P(("dp", "pipe")),
            P(("dp", "pipe"), None),
            P(("dp", "pipe"), None),
            P(("dp", "pipe")),
            P(("dp", "pipe")),
            P(("dp", "pipe"), "tensor"),
            P("pipe", None),
            P("pipe", None, "tensor"),
            P("pipe", None, "tensor"),
            P("pipe", None, "tensor"),
            P("pipe", "tensor", None),
            P(),
        ),
        out_specs=(P(None, "tensor"), P(("dp", "pipe"), None)),
        check_vma=False,
    )
```

profile of v0, /device:TPU:0, one launch (start us, length us, event | category | flops | bytes accessed | tf_op | source)
XLA Modules:
  0.0 681.9 jit_solution(12424556584828293104)
XLA Ops:
  0.6 33.8 %all-gather.1 = s32[32,1,32]{2,1,0:T(1,128)S(1)} all-gather(s32[1,1,32]{2,1,0:T(1,128)} %bitcast.148), channel_id=1, replica_groups=mesh['dp'=8,'pipe'=4,'tensor'=4] {'dp','pipe'}, dimensions={0}, use_global_device_ids=true | all-gather | bytes 4224 | tf_op jit(solution)/shard_map/all_gather | solution.py:103
  34.4 36.5 %all-gather = s32[32,2,32]{2,1,0:T(2,128)S(1)} all-gather(s32[1,2,32]{2,1,0:T(2,128)} %bitcast.144), channel_id=1, replica_groups=mesh['dp'=8,'pipe'=4,'tensor'=4] {'dp','pipe'}, dimensions={0}, use_global_device_ids=true | all-gather | bytes 8448 | tf_op jit(solution)/shard_map/all_gather | solution.py:102
  71.2 18.7 %gather_fusion = bf16[3072,1024]{1,0:T(8,128)(2,1)} fusion(bf16[2004,1024]{1,0:T(8,128)(2,1)} %param.21, s32[3072]{0:T(1024)S(1)} %broadcast_clamp_fusion.1), kind=kCustom, calls=%fused_computation | custom fusion | bytes 12595200 | tf_op jit(solution)/shard_map/jit(_take)/gather | solution.py:112
  89.9 7.0 %select_select_fusion = bf16[32,96,1024]{2,1,0:T(8,128)(2,1)} fusion(bf16[32,96,1024]{2,1,0:T(8,128)(2,1)} %bitcast.128, pred[32,96]{1,0:T(8,128)(4,1)S(1)} %get-tuple-element.312, pred[32,96]{1,0:T(8,128)(4,1)S(1)} %get-tuple-element.322), kind=kLoop, calls=%fused_computation.56 | loop fusion | flops 6291456 | bytes 12589056 | tf_op jit(solution)/shard_map/jit(_where)/select_n | solution.py:113
  96.9 5.7 all-to-all-start.2
  105.7 79.5 %all-reduce.2 = (s32[64]{0:T(128)S(1)}, s32[32]{0:T(128)S(1)}) all-reduce(s32[64]{0:T(128)S(1)} %dynamic-update-slice, s32[32]{0:T(128)S(1)} %dynamic-update-slice.1), channel_id=1, replica_groups=mesh['dp'=8,'pipe'=4,'tensor'=4] {'dp','pipe'}, use_global_device_ids=true, to_apply=%add | all-reduce | flops 96 | bytes 768
  185.3 11.6 %pad_maximum_fusion = bf16[4096,1536]{1,0:T(8,128)(2,1)} fusion(bf16[4096,256]{1,0:T(8,128)(2,1)S(1)} %bitcast.135, bf16[4096,256]{1,0:T(8,128)(2,1)} %bitcast.136, bf16[4096,1024]{1,0:T(8,128)(2,1)} %bitcast.129), kind=kLoop, calls=%fused_computation.55 | loop fusion | flops 37748736 | bytes 25165824 | tf_op jit(solution)/shard_map/concatenate | solution.py:127
  201.1 409.0 %while.16 = (s32[]{:T(128)}, bf16[96,1024]{1,0:T(8,128)(2,1)S(1)}, s32[]{:T(128)}, f32[1,4096]{1,0:T(1,128)S(1)}, bf16[4096,1536]{1,0:T(8,128)(2,1)}, /*index=5*...) while((s32[]{:T(128)}, bf16[96,1024]{1,0:T(8,128)(2,1)S(1)}, ...), condition=%wide.region_6.7_spmd.clone, body=%wide.region_1.0_spmd.clone.sunk | while | flops 2038168704 | bytes 45535072 | solution.py:179
  202.2 5.3 all-to-all-start
  209.2 10.1 %all-to-all-done = bf16[4,96,1024]{2,1,0:T(8,128)(2,1)S(1)} async-done(((bf16[4,96,1024]{2,1,0:T(8,128)(2,1)}), bf16[4,96,1024]{2,1,0:T(8,128)(2,1)S(1)}, u32[]{:S(2)}, u32[]{:S(2)}) %all-to-all-start) | async-done | bytes 786464 | tf_op jit(solution)/shard_map/while/body/eval_jaxpr/all_to_all | solution.py:23
  219.9 6.8 fusion.84
  229.0 4.8 convolution_convert_fusion.4
  238.3 11.0 %all-to-all-done.1 = bf16[4,96,1024]{2,1,0:T(8,128)(2,1)S(1)} async-done(((bf16[4,96,1024]{2,1,0:T(8,128)(2,1)}), bf16[4,96,1024]{2,1,0:T(8,128)(2,1)S(1)}, u32[]{:S(2)}, u32[]{:S(2)}) %all-to-all-start.1) | async-done | bytes 786464 | tf_op jit(solution)/shard_map/while/body/eval_jaxpr/all_to_all | solution.py:38
  250.6 5.8 collective-permute-done
  262.7 7.7 %all-to-all-done = bf16[4,96,1024]{2,1,0:T(8,128)(2,1)S(1)} async-done(((bf16[4,96,1024]{2,1,0:T(8,128)(2,1)}), bf16[4,96,1024]{2,1,0:T(8,128)(2,1)S(1)}, u32[]{:S(2)}, u32[]{:S(2)}) %all-to-all-start) | async-done | bytes 786464 | tf_op jit(solution)/shard_map/while/body/eval_jaxpr/all_to_all | solution.py:23
  271.0 6.8 fusion.84
  289.3 9.4 %all-to-all-done.1 = bf16[4,96,1024]{2,1,0:T(8,128)(2,1)S(1)} async-done(((bf16[4,96,1024]{2,1,0:T(8,128)(2,1)}), bf16[4,96,1024]{2,1,0:T(8,128)(2,1)S(1)}, u32[]{:S(2)}, u32[]{:S(2)}) %all-to-all-start.1) | async-done | bytes 786464 | tf_op jit(solution)/shard_map/while/body/eval_jaxpr/all_to_all | solution.py:38
  299.0 6.9 %collective-permute-done = bf16[96,1024]{1,0:T(8,128)(2,1)S(1)} collective-permute-done((bf16[96,1024]{1,0:T(8,128)(2,1)S(1)}, bf16[96,1024]{1,0:T(8,128)(2,1)S(1)}, u32[]{:S(2)}, u32[]{:S(2)}) %collective-permute-start) | collective-permute-done | bytes 196640 | tf_op jit(solution)/shard_map/while/body/eval_jaxpr/ppermute | solution.py:45
  312.2 7.7 %all-to-all-done = bf16[4,96,1024]{2,1,0:T(8,128)(2,1)S(1)} async-done(((bf16[4,96,1024]{2,1,0:T(8,128)(2,1)}), bf16[4,96,1024]{2,1,0:T(8,128)(2,1)S(1)}, u32[]{:S(2)}, u32[]{:S(2)}) %all-to-all-start) | async-done | bytes 786464 | tf_op jit(solution)/shard_map/while/body/eval_jaxpr/all_to_all | solution.py:23
  320.4 6.8 fusion.84
  329.5 4.8 convolution_convert_fusion.4
  338.8 9.4 %all-to-all-done.1 = bf16[4,96,1024]{2,1,0:T(8,128)(2,1)S(1)} async-done(((bf16[4,96,1024]{2,1,0:T(8,128)(2,1)}), bf16[4,96,1024]{2,1,0:T(8,128)(2,1)S(1)}, u32[]{:S(2)}, u32[]{:S(2)}) %all-to-all-start.1) | async-done | bytes 786464 | tf_op jit(solution)/shard_map/while/body/eval_jaxpr/all_to_all | solution.py:38
  348.5 6.9 %collective-permute-done = bf16[96,1024]{1,0:T(8,128)(2,1)S(1)} collective-permute-done((bf16[96,1024]{1,0:T(8,128)(2,1)S(1)}, bf16[96,1024]{1,0:T(8,128)(2,1)S(1)}, u32[]{:S(2)}, u32[]{:S(2)}) %collective-permute-start) | collective-permute-done | bytes 196640 | tf_op jit(solution)/shard_map/while/body/eval_jaxpr/ppermute | solution.py:45
  361.7 7.7 %all-to-all-done = bf16[4,96,1024]{2,1,0:T(8,128)(2,1)S(1)} async-done(((bf16[4,96,1024]{2,1,0:T(8,128)(2,1)}), bf16[4,96,1024]{2,1,0:T(8,128)(2,1)S(1)}, u32[]{:S(2)}, u32[]{:S(2)}) %all-to-all-start) | async-done | bytes 786464 | tf_op jit(solution)/shard_map/while/body/eval_jaxpr/all_to_all | solution.py:23
  369.9 6.8 fusion.84
  388.3 9.4 %all-to-all-done.1 = bf16[4,96,1024]{2,1,0:T(8,128)(2,1)S(1)} async-done(((bf16[4,96,1024]{2,1,0:T(8,128)(2,1)}), bf16[4,96,1024]{2,1,0:T(8,128)(2,1)S(1)}, u32[]{:S(2)}, u32[]{:S(2)}) %all-to-all-start.1) | async-done | bytes 786464 | tf_op jit(solution)/shard_map/while/body/eval_jaxpr/all_to_all | solution.py:38
  398.0 6.9 %collective-permute-done = bf16[96,1024]{1,0:T(8,128)(2,1)S(1)} collective-permute-done((bf16[96,1024]{1,0:T(8,128)(2,1)S(1)}, bf16[96,1024]{1,0:T(8,128)(2,1)S(1)}, u32[]{:S(2)}, u32[]{:S(2)}) %collective-permute-start) | collective-permute-done | bytes 196640 | tf_op jit(solution)/shard_map/while/body/eval_jaxpr/ppermute | solution.py:45
  411.2 7.7 %all-to-all-done = bf16[4,96,1024]{2,1,0:T(8,128)(2,1)S(1)} async-done(((bf16[4,96,1024]{2,1,0:T(8,128)(2,1)}), bf16[4,96,1024]{2,1,0:T(8,128)(2,1)S(1)}, u32[]{:S(2)}, u32[]{:S(2)}) %all-to-all-start) | async-done | bytes 786464 | tf_op jit(solution)/shard_map/while/body/eval_jaxpr/all_to_all | solution.py:23
  419.4 6.8 fusion.84
  437.8 10.7 %all-to-all-done.1 = bf16[4,96,1024]{2,1,0:T(8,128)(2,1)S(1)} async-done(((bf16[4,96,1024]{2,1,0:T(8,128)(2,1)}), bf16[4,96,1024]{2,1,0:T(8,128)(2,1)S(1)}, u32[]{:S(2)}, u32[]{:S(2)}) %all-to-all-start.1) | async-done | bytes 786464 | tf_op jit(solution)/shard_map/while/body/eval_jaxpr/all_to_all | solution.py:38
  448.8 6.9 %collective-permute-done = bf16[96,1024]{1,0:T(8,128)(2,1)S(1)} collective-permute-done((bf16[96,1024]{1,0:T(8,128)(2,1)S(1)}, bf16[96,1024]{1,0:T(8,128)(2,1)S(1)}, u32[]{:S(2)}, u32[]{:S(2)}) %collective-permute-start) | collective-permute-done | bytes 196640 | tf_op jit(solution)/shard_map/while/body/eval_jaxpr/ppermute | solution.py:45
  462.0 7.7 %all-to-all-done = bf16[4,96,1024]{2,1,0:T(8,128)(2,1)S(1)} async-done(((bf16[4,96,1024]{2,1,0:T(8,128)(2,1)}), bf16[4,96,1024]{2,1,0:T(8,128)(2,1)S(1)}, u32[]{:S(2)}, u32[]{:S(2)}) %all-to-all-start) | async-done | bytes 786464 | tf_op jit(solution)/shard_map/while/body/eval_jaxpr/all_to_all | solution.py:23
  470.2 6.8 fusion.84
  488.6 13.1 %all-to-all-done.1 = bf16[4,96,1024]{2,1,0:T(8,128)(2,1)S(1)} async-done(((bf16[4,96,1024]{2,1,0:T(8,128)(2,1)}), bf16[4,96,1024]{2,1,0:T(8,128)(2,1)S(1)}, u32[]{:S(2)}, u32[]{:S(2)}) %all-to-all-start.1) | async-done | bytes 786464 | tf_op jit(solution)/shard_map/while/body/eval_jaxpr/all_to_all | solution.py:38
  502.0 6.9 %collective-permute-done = bf16[96,1024]{1,0:T(8,128)(2,1)S(1)} collective-permute-done((bf16[96,1024]{1,0:T(8,128)(2,1)S(1)}, bf16[96,1024]{1,0:T(8,128)(2,1)S(1)}, u32[]{:S(2)}, u32[]{:S(2)}) %collective-permute-start) | collective-permute-done | bytes 196640 | tf_op jit(solution)/shard_map/while/body/eval_jaxpr/ppermute | solution.py:45
  515.1 7.7 %all-to-all-done = bf16[4,96,1024]{2,1,0:T(8,128)(2,1)S(1)} async-done(((bf16[4,96,1024]{2,1,0:T(8,128)(2,1)}), bf16[4,96,1024]{2,1,0:T(8,128)(2,1)S(1)}, u32[]{:S(2)}, u32[]{:S(2)}) %all-to-all-start) | async-done | bytes 786464 | tf_op jit(solution)/shard_map/while/body/eval_jaxpr/all_to_all | solution.py:23
  523.4 6.8 fusion.84
  541.8 10.0 %all-to-all-done.1 = bf16[4,96,1024]{2,1,0:T(8,128)(2,1)S(1)} async-done(((bf16[4,96,1024]{2,1,0:T(8,128)(2,1)}), bf16[4,96,1024]{2,1,0:T(8,128)(2,1)S(1)}, u32[]{:S(2)}, u32[]{:S(2)}) %all-to-all-start.1) | async-done | bytes 786464 | tf_op jit(solution)/shard_map/while/body/eval_jaxpr/all_to_all | solution.py:38
  552.0 6.9 %collective-permute-done = bf16[96,1024]{1,0:T(8,128)(2,1)S(1)} collective-permute-done((bf16[96,1024]{1,0:T(8,128)(2,1)S(1)}, bf16[96,1024]{1,0:T(8,128)(2,1)S(1)}, u32[]{:S(2)}, u32[]{:S(2)}) %collective-permute-start) | collective-permute-done | bytes 196640 | tf_op jit(solution)/shard_map/while/body/eval_jaxpr/ppermute | solution.py:45
  565.2 9.5 %all-to-all-done = bf16[4,96,1024]{2,1,0:T(8,128)(2,1)S(1)} async-done(((bf16[4,96,1024]{2,1,0:T(8,128)(2,1)}), bf16[4,96,1024]{2,1,0:T(8,128)(2,1)S(1)}, u32[]{:S(2)}, u32[]{:S(2)}) %all-to-all-start) | async-done | bytes 786464 | tf_op jit(solution)/shard_map/while/body/eval_jaxpr/all_to_all | solution.py:23
  575.2 6.8 fusion.84
  593.6 9.4 %all-to-all-done.1 = bf16[4,96,1024]{2,1,0:T(8,128)(2,1)S(1)} async-done(((bf16[4,96,1024]{2,1,0:T(8,128)(2,1)}), bf16[4,96,1024]{2,1,0:T(8,128)(2,1)S(1)}, u32[]{:S(2)}, u32[]{:S(2)}) %all-to-all-start.1) | async-done | bytes 786464 | tf_op jit(solution)/shard_map/while/body/eval_jaxpr/all_to_all | solution.py:38
  603.3 6.9 %collective-permute-done = bf16[96,1024]{1,0:T(8,128)(2,1)S(1)} collective-permute-done((bf16[96,1024]{1,0:T(8,128)(2,1)S(1)}, bf16[96,1024]{1,0:T(8,128)(2,1)S(1)}, u32[]{:S(2)}, u32[]{:S(2)}) %collective-permute-start) | collective-permute-done | bytes 196640 | tf_op jit(solution)/shard_map/while/body/eval_jaxpr/ppermute | solution.py:45
  614.9 9.2 %all-to-all-done.3 = bf16[4,96,1024]{2,1,0:T(8,128)(2,1)S(1)} async-done(((bf16[4,96,1024]{2,1,0:T(8,128)(2,1)}), bf16[4,96,1024]{2,1,0:T(8,128)(2,1)S(1)}, u32[]{:S(2)}, u32[]{:S(2)}) %all-to-all-start.3) | async-done | bytes 786464 | tf_op jit(solution)/shard_map/all_to_all | solution.py:23
  624.7 5.5 all-to-all-start.5
  631.5 6.0 all-to-all-done.5
  643.8 27.6 %all-to-all-done.4 = bf16[32,32,1024]{2,1,0:T(8,128)(2,1)S(1)} async-done(((bf16[32,32,1024]{2,1,0:T(8,128)(2,1)}), bf16[32,32,1024]{2,1,0:T(8,128)(2,1)S(1)}, u32[]{:S(2)}, u32[]{:S(2)}) %all-to-all-start.4) | async-done | bytes 2097184 | tf_op jit(solution)/shard_map/all_to_all | solution.py:23
  672.4 8.9 %psum.7 = f32[1,16]{1,0:T(1,128)S(1)} all-reduce(f32[1,16]{1,0:T(1,128)S(1)} %bitcast.147), channel_id=1, replica_groups=mesh['dp'=8,'pipe'=4,'tensor'=4] {'tensor'}, use_global_device_ids=true, to_apply=%region_13.14 | all-reduce | flops 16 | bytes 128 | tf_op jit(solution)/shard_map/psum | solution.py:208
  (326 shorter events, 156.1 us)
Async XLA Ops:
  96.9 6.4 copy-start.5
  96.9 7.8 %copy-start.4 = (s32[2]{0:T(128)S(1)}, s32[2]{0:T(128)}, u32[]{:S(2)}) copy-start(s32[2]{0:T(128)} %param.16) | copy-start | bytes 28
  96.9 88.4 %copy-start = (bf16[1,4096,256]{2,1,0:T(8,128)(2,1)S(1)}, bf16[1,4096,256]{2,1,0:T(8,128)(2,1)}, u32[]{:S(2)}) copy-start(bf16[1,4096,256]{2,1,0:T(8,128)(2,1)} %param.25) | copy-start | bytes 6291460
  96.9 99.9 %all-to-all-start.2 = ((bf16[32,96,1024]{2,1,0:T(8,128)(2,1)}), bf16[32,96,1024]{2,1,0:T(8,128)(2,1)}, u32[]{:S(2)}, u32[]{:S(2)}) async-start(bf16[32,96,1024]{2,1,0:T(8,128)(2,1)} %select_select_fusion), calls=%async_computation.2 | async-start | bytes 12582912 | tf_op jit(solution)/shard_map/all_to_all | solution.py:114
  196.8 4.3 copy-start.1
  201.1 413.6 %copy-start.3 = (s32[2,1]{0,1:T(1,128)S(1)}, s32[2,1]{0,1:T(1,128)}, u32[]{:S(2)}) copy-start(s32[2,1]{0,1:T(1,128)} %param.17) | copy-start | bytes 28
  202.2 17.2 %all-to-all-start = ((bf16[4,96,1024]{2,1,0:T(8,128)(2,1)}), bf16[4,96,1024]{2,1,0:T(8,128)(2,1)S(1)}, u32[]{:S(2)}, u32[]{:S(2)}) async-start(bf16[4,96,1024]{2,1,0:T(8,128)(2,1)} %broadcast_in_dim.169), calls=%async_computation | async-start | bytes 1572864 | tf_op jit(solution)/shard_map/while/body/eval_jaxpr/all_to_all | solution.py:23
  234.8 14.5 %all-to-all-start.1 = ((bf16[4,96,1024]{2,1,0:T(8,128)(2,1)}), bf16[4,96,1024]{2,1,0:T(8,128)(2,1)S(1)}, u32[]{:S(2)}, u32[]{:S(2)}) async-start(bf16[4,96,1024]{2,1,0:T(8,128)(2,1)} %bitcast.122), calls=%async_computation.1 | async-start | bytes 1572864 | tf_op jit(solution)/shard_map/while/body/eval_jaxpr/all_to_all | solution.py:38
  249.5 6.9 %collective-permute-start = (bf16[96,1024]{1,0:T(8,128)(2,1)S(1)}, bf16[96,1024]{1,0:T(8,128)(2,1)S(1)}, u32[]{:S(2)}, u32[]{:S(2)}) collective-permute-start(bf16[96,1024]{1,0:T(8,128)(2,1)S(1)} %fusion.89), channel_id=1, source_target_pairs={{12,0},{0,4},{4,8},{8,12},{13,1},{1,5},{5,9},{9,13},{14,2},{2,6},{... | collective-permute-start | bytes 589832 | tf_op jit(solution)/shard_map/while/body/eval_jaxpr/ppermute | solution.py:45
  257.4 13.0 %all-to-all-start = ((bf16[4,96,1024]{2,1,0:T(8,128)(2,1)}), bf16[4,96,1024]{2,1,0:T(8,128)(2,1)S(1)}, u32[]{:S(2)}, u32[]{:S(2)}) async-start(bf16[4,96,1024]{2,1,0:T(8,128)(2,1)} %broadcast_in_dim.169), calls=%async_computation | async-start | bytes 1572864 | tf_op jit(solution)/shard_map/while/body/eval_jaxpr/all_to_all | solution.py:23
  285.8 13.0 %all-to-all-start.1 = ((bf16[4,96,1024]{2,1,0:T(8,128)(2,1)}), bf16[4,96,1024]{2,1,0:T(8,128)(2,1)S(1)}, u32[]{:S(2)}, u32[]{:S(2)}) async-start(bf16[4,96,1024]{2,1,0:T(8,128)(2,1)} %bitcast.122), calls=%async_computation.1 | async-start | bytes 1572864 | tf_op jit(solution)/shard_map/while/body/eval_jaxpr/all_to_all | solution.py:38
  299.0 6.9 %collective-permute-start = (bf16[96,1024]{1,0:T(8,128)(2,1)S(1)}, bf16[96,1024]{1,0:T(8,128)(2,1)S(1)}, u32[]{:S(2)}, u32[]{:S(2)}) collective-permute-start(bf16[96,1024]{1,0:T(8,128)(2,1)S(1)} %fusion.89), channel_id=1, source_target_pairs={{12,0},{0,4},{4,8},{8,12},{13,1},{1,5},{5,9},{9,13},{14,2},{2,6},{... | collective-permute-start | bytes 589832 | tf_op jit(solution)/shard_map/while/body/eval_jaxpr/ppermute | solution.py:45
  306.9 13.0 %all-to-all-start = ((bf16[4,96,1024]{2,1,0:T(8,128)(2,1)}), bf16[4,96,1024]{2,1,0:T(8,128)(2,1)S(1)}, u32[]{:S(2)}, u32[]{:S(2)}) async-start(bf16[4,96,1024]{2,1,0:T(8,128)(2,1)} %broadcast_in_dim.169), calls=%async_computation | async-start | bytes 1572864 | tf_op jit(solution)/shard_map/while/body/eval_jaxpr/all_to_all | solution.py:23
  335.3 13.0 %all-to-all-start.1 = ((bf16[4,96,1024]{2,1,0:T(8,128)(2,1)}), bf16[4,96,1024]{2,1,0:T(8,128)(2,1)S(1)}, u32[]{:S(2)}, u32[]{:S(2)}) async-start(bf16[4,96,1024]{2,1,0:T(8,128)(2,1)} %bitcast.122), calls=%async_computation.1 | async-start | bytes 1572864 | tf_op jit(solution)/shard_map/while/body/eval_jaxpr/all_to_all | solution.py:38
  348.5 6.9 %collective-permute-start = (bf16[96,1024]{1,0:T(8,128)(2,1)S(1)}, bf16[96,1024]{1,0:T(8,128)(2,1)S(1)}, u32[]{:S(2)}, u32[]{:S(2)}) collective-permute-start(bf16[96,1024]{1,0:T(8,128)(2,1)S(1)} %fusion.89), channel_id=1, source_target_pairs={{12,0},{0,4},{4,8},{8,12},{13,1},{1,5},{5,9},{9,13},{14,2},{2,6},{... | collective-permute-start | bytes 589832 | tf_op jit(solution)/shard_map/while/body/eval_jaxpr/ppermute | solution.py:45
  356.4 13.0 %all-to-all-start = ((bf16[4,96,1024]{2,1,0:T(8,128)(2,1)}), bf16[4,96,1024]{2,1,0:T(8,128)(2,1)S(1)}, u32[]{:S(2)}, u32[]{:S(2)}) async-start(bf16[4,96,1024]{2,1,0:T(8,128)(2,1)} %broadcast_in_dim.169), calls=%async_computation | async-start | bytes 1572864 | tf_op jit(solution)/shard_map/while/body/eval_jaxpr/all_to_all | solution.py:23
  384.8 13.0 %all-to-all-start.1 = ((bf16[4,96,1024]{2,1,0:T(8,128)(2,1)}), bf16[4,96,1024]{2,1,0:T(8,128)(2,1)S(1)}, u32[]{:S(2)}, u32[]{:S(2)}) async-start(bf16[4,96,1024]{2,1,0:T(8,128)(2,1)} %bitcast.122), calls=%async_computation.1 | async-start | bytes 1572864 | tf_op jit(solution)/shard_map/while/body/eval_jaxpr/all_to_all | solution.py:38
  397.9 6.9 %collective-permute-start = (bf16[96,1024]{1,0:T(8,128)(2,1)S(1)}, bf16[96,1024]{1,0:T(8,128)(2,1)S(1)}, u32[]{:S(2)}, u32[]{:S(2)}) collective-permute-start(bf16[96,1024]{1,0:T(8,128)(2,1)S(1)} %fusion.89), channel_id=1, source_target_pairs={{12,0},{0,4},{4,8},{8,12},{13,1},{1,5},{5,9},{9,13},{14,2},{2,6},{... | collective-permute-start | bytes 589832 | tf_op jit(solution)/shard_map/while/body/eval_jaxpr/ppermute | solution.py:45
  405.9 13.0 %all-to-all-start = ((bf16[4,96,1024]{2,1,0:T(8,128)(2,1)}), bf16[4,96,1024]{2,1,0:T(8,128)(2,1)S(1)}, u32[]{:S(2)}, u32[]{:S(2)}) async-start(bf16[4,96,1024]{2,1,0:T(8,128)(2,1)} %broadcast_in_dim.169), calls=%async_computation | async-start | bytes 1572864 | tf_op jit(solution)/shard_map/while/body/eval_jaxpr/all_to_all | solution.py:23
  434.3 14.2 %all-to-all-start.1 = ((bf16[4,96,1024]{2,1,0:T(8,128)(2,1)}), bf16[4,96,1024]{2,1,0:T(8,128)(2,1)S(1)}, u32[]{:S(2)}, u32[]{:S(2)}) async-start(bf16[4,96,1024]{2,1,0:T(8,128)(2,1)} %bitcast.122), calls=%async_computation.1 | async-start | bytes 1572864 | tf_op jit(solution)/shard_map/while/body/eval_jaxpr/all_to_all | solution.py:38
  448.7 6.9 %collective-permute-start = (bf16[96,1024]{1,0:T(8,128)(2,1)S(1)}, bf16[96,1024]{1,0:T(8,128)(2,1)S(1)}, u32[]{:S(2)}, u32[]{:S(2)}) collective-permute-start(bf16[96,1024]{1,0:T(8,128)(2,1)S(1)} %fusion.89), channel_id=1, source_target_pairs={{12,0},{0,4},{4,8},{8,12},{13,1},{1,5},{5,9},{9,13},{14,2},{2,6},{... | collective-permute-start | bytes 589832 | tf_op jit(solution)/shard_map/while/body/eval_jaxpr/ppermute | solution.py:45
  456.7 13.0 %all-to-all-start = ((bf16[4,96,1024]{2,1,0:T(8,128)(2,1)}), bf16[4,96,1024]{2,1,0:T(8,128)(2,1)S(1)}, u32[]{:S(2)}, u32[]{:S(2)}) async-start(bf16[4,96,1024]{2,1,0:T(8,128)(2,1)} %broadcast_in_dim.169), calls=%async_computation | async-start | bytes 1572864 | tf_op jit(solution)/shard_map/while/body/eval_jaxpr/all_to_all | solution.py:23
  485.0 16.7 %all-to-all-start.1 = ((bf16[4,96,1024]{2,1,0:T(8,128)(2,1)}), bf16[4,96,1024]{2,1,0:T(8,128)(2,1)S(1)}, u32[]{:S(2)}, u32[]{:S(2)}) async-start(bf16[4,96,1024]{2,1,0:T(8,128)(2,1)} %bitcast.122), calls=%async_computation.1 | async-start | bytes 1572864 | tf_op jit(solution)/shard_map/while/body/eval_jaxpr/all_to_all | solution.py:38
  501.9 6.9 %collective-permute-start = (bf16[96,1024]{1,0:T(8,128)(2,1)S(1)}, bf16[96,1024]{1,0:T(8,128)(2,1)S(1)}, u32[]{:S(2)}, u32[]{:S(2)}) collective-permute-start(bf16[96,1024]{1,0:T(8,128)(2,1)S(1)} %fusion.89), channel_id=1, source_target_pairs={{12,0},{0,4},{4,8},{8,12},{13,1},{1,5},{5,9},{9,13},{14,2},{2,6},{... | collective-permute-start | bytes 589832 | tf_op jit(solution)/shard_map/while/body/eval_jaxpr/ppermute | solution.py:45
  509.9 13.0 %all-to-all-start = ((bf16[4,96,1024]{2,1,0:T(8,128)(2,1)}), bf16[4,96,1024]{2,1,0:T(8,128)(2,1)S(1)}, u32[]{:S(2)}, u32[]{:S(2)}) async-start(bf16[4,96,1024]{2,1,0:T(8,128)(2,1)} %broadcast_in_dim.169), calls=%async_computation | async-start | bytes 1572864 | tf_op jit(solution)/shard_map/while/body/eval_jaxpr/all_to_all | solution.py:23
  538.2 13.5 %all-to-all-start.1 = ((bf16[4,96,1024]{2,1,0:T(8,128)(2,1)}), bf16[4,96,1024]{2,1,0:T(8,128)(2,1)S(1)}, u32[]{:S(2)}, u32[]{:S(2)}) async-start(bf16[4,96,1024]{2,1,0:T(8,128)(2,1)} %bitcast.122), calls=%async_computation.1 | async-start | bytes 1572864 | tf_op jit(solution)/shard_map/while/body/eval_jaxpr/all_to_all | solution.py:38
  551.9 6.9 %collective-permute-start = (bf16[96,1024]{1,0:T(8,128)(2,1)S(1)}, bf16[96,1024]{1,0:T(8,128)(2,1)S(1)}, u32[]{:S(2)}, u32[]{:S(2)}) collective-permute-start(bf16[96,1024]{1,0:T(8,128)(2,1)S(1)} %fusion.89), channel_id=1, source_target_pairs={{12,0},{0,4},{4,8},{8,12},{13,1},{1,5},{5,9},{9,13},{14,2},{2,6},{... | collective-permute-start | bytes 589832 | tf_op jit(solution)/shard_map/while/body/eval_jaxpr/ppermute | solution.py:45
  559.9 14.7 %all-to-all-start = ((bf16[4,96,1024]{2,1,0:T(8,128)(2,1)}), bf16[4,96,1024]{2,1,0:T(8,128)(2,1)S(1)}, u32[]{:S(2)}, u32[]{:S(2)}) async-start(bf16[4,96,1024]{2,1,0:T(8,128)(2,1)} %broadcast_in_dim.169), calls=%async_computation | async-start | bytes 1572864 | tf_op jit(solution)/shard_map/while/body/eval_jaxpr/all_to_all | solution.py:23
  590.0 13.0 %all-to-all-start.1 = ((bf16[4,96,1024]{2,1,0:T(8,128)(2,1)}), bf16[4,96,1024]{2,1,0:T(8,128)(2,1)S(1)}, u32[]{:S(2)}, u32[]{:S(2)}) async-start(bf16[4,96,1024]{2,1,0:T(8,128)(2,1)} %bitcast.122), calls=%async_computation.1 | async-start | bytes 1572864 | tf_op jit(solution)/shard_map/while/body/eval_jaxpr/all_to_all | solution.py:38
  603.2 6.9 %collective-permute-start = (bf16[96,1024]{1,0:T(8,128)(2,1)S(1)}, bf16[96,1024]{1,0:T(8,128)(2,1)S(1)}, u32[]{:S(2)}, u32[]{:S(2)}) collective-permute-start(bf16[96,1024]{1,0:T(8,128)(2,1)S(1)} %fusion.89), channel_id=1, source_target_pairs={{12,0},{0,4},{4,8},{8,12},{13,1},{1,5},{5,9},{9,13},{14,2},{2,6},{... | collective-permute-start | bytes 589832 | tf_op jit(solution)/shard_map/while/body/eval_jaxpr/ppermute | solution.py:45
  611.1 13.0 %all-to-all-start.3 = ((bf16[4,96,1024]{2,1,0:T(8,128)(2,1)}), bf16[4,96,1024]{2,1,0:T(8,128)(2,1)S(1)}, u32[]{:S(2)}, u32[]{:S(2)}) async-start(bf16[4,96,1024]{2,1,0:T(8,128)(2,1)} %broadcast_in_dim.128), calls=%async_computation.3 | async-start | bytes 1572864 | tf_op jit(solution)/shard_map/all_to_all | solution.py:23
  614.6 16.2 %dynamic-slice-start = ((f32[4096]{0:T(1024)}, s32[]{:T(128)}), f32[1024]{0:T(1024)S(1)}, s32[]{:S(2)}) async-start(f32[4096]{0:T(1024)} %param.27, s32[]{:T(128)} %select_n.118), calls=%async_computation.6 | async-start | bytes 8704 | tf_op jit(solution)/shard_map/dynamic_slice | solution.py:180
  624.7 12.8 %all-to-all-start.5 = ((bf16[32,1,32]{2,1,0:T(2,128)(2,1)}), bf16[32,1,32]{2,1,0:T(2,128)(2,1)S(1)}, u32[]{:S(2)}, u32[]{:S(2)}) async-start(bf16[32,1,32]{2,1,0:T(2,128)(2,1)} %broadcast_in_dim.130), calls=%async_computation.5 | async-start | bytes 32768 | tf_op jit(solution)/shard_map/all_to_all | solution.py:23
  639.1 32.3 %all-to-all-start.4 = ((bf16[32,32,1024]{2,1,0:T(8,128)(2,1)}), bf16[32,32,1024]{2,1,0:T(8,128)(2,1)S(1)}, u32[]{:S(2)}, u32[]{:S(2)}) async-start(bf16[32,32,1024]{2,1,0:T(8,128)(2,1)} %broadcast_in_dim.129), calls=%async_computation.4 | async-start | bytes 4194304 | tf_op jit(solution)/shard_map/all_to_all | solution.py:23
  671.9 10.0 %copy-start.2 = (f32[32,1024]{1,0:T(8,128)}, f32[32,1024]{1,0:T(8,128)S(1)}, u32[]{:S(2)}) copy-start(f32[32,1024]{1,0:T(8,128)S(1)} %broadcast_divide_fusion) | copy-start | bytes 393220
where the time goes:
time: 684 us; the launch traced here: 682 us
  waiting for transfers between devices  245 us (36%)
  blocking collectives  159 us (23%)
  matrix products  104 us (15%)
  starting transfers between devices  78.1 us (11%)
  local copies, waits for them, and re-layouts  51.8 us (8%)
  other arithmetic  39.9 us (6%)
    all_to_all x11, waiting for transfers between devices, sent_to_all(): return lax.all_to_all(copies, axis, split_axis=0, concat_axis=0, tiled=True)  108 us
    all_to_all x8, waiting for transfers between devices, sum_at_owner(): lax.all_to_all(split_up(shard, dim, length), axis, 0, 0, tiled=True)  82.5 us
    unnamed x1, blocking collectives  79.5 us
    dot_general x8, matrix products, section_block(): projected = jnp.dot(normed, w_in, preferred_element_type=jnp.float32)  54.2 us
    ppermute x8, waiting for transfers between devices, passed_along(): return lax.ppermute(block, axis, route)  53.9 us
    all_to_all x11, starting transfers between devices, sent_to_all(): return lax.all_to_all(copies, axis, split_axis=0, concat_axis=0, tiled=True)  42.8 us
    dot_general x8, matrix products, section_block(): partial_out = jnp.dot(mixed, out_proj, preferred_element_type=jnp.float32)  38.7 us
    all_gather x1, blocking collectives, shards(): lax.all_gather(support_tokens, ('dp', 'pipe'), axis=0, tiled=True)  36.5 us
  transfers between devices with their start and end apart: 28, of which 27 were waited for; matrix products, arithmetic and copies ran while one was open for 4% of the time, Pallas kernels for 0%

commit v1 on v0

--- a/solution.py
+++ b/solution.py
@@ -10,6 +10,14 @@
 EPISODES = 2
 epsilon = 1e-05
 rotary_base = 500000.0
+
+
+def gather_from_all(shard, axis, dim):
+    size = lax.axis_size(axis)
+    repeats = [size if d == dim else 1 for d in range(shard.ndim)]
+    return lax.all_to_all(
+        jnp.tile(shard, repeats), axis, split_axis=dim, concat_axis=dim, tiled=True
+    )
 
 
 def in_order(blocks, dim):
@@ -99,7 +107,7 @@
     table_rows, width = embedding.shape
     column_start = lax.axis_index("tensor") * width
     all_support, all_query, every_sup_len, every_qry_len = (
-        lax.all_gather(support_tokens, ("dp", "pipe"), axis=0, tiled=True),
+        gather_from_all(support_tokens, ("dp", "pipe"), 0),
         lax.all_gather(query_tokens, ("dp", "pipe"), axis=0, tiled=True),
         lax.all_gather(support_lengths, ("dp", "pipe"), axis=0, tiled=True),
         lax.all_gather(query_lengths, ("dp", "pipe"), axis=0, tiled=True),

time: 684 us -> 656 us (0.959)
  blocking collectives: 159 us -> 123 us
    all_gather x1 -> x0, blocking collectives: 36.5 us -> none  [shards(): lax.all_gather(support_tokens, ('dp', 'pipe'), axis=0, tiled=True)]
    all_to_all x0 -> x1, starting transfers between devices: none -> 7.43 us  [gather_from_all(): lax.all_to_all(jnp.tile(shard, repeats), axis, split_axis=dim, concat_axi...]
  transfers between devices with their start and end apart: 28 -> 29, of which waited for: 27 -> 27; matrix products, arithmetic and copies ran while one was open for 4% -> 4% of each run, Pallas kernels for 0% -> 0%
where the time goes in v1:
time: 656 us; the launch traced here: 654 us
  waiting for transfers between devices  245 us (37%)
  blocking collectives  123 us (19%)
  matrix products  104 us (16%)
  starting transfers between devices  84.9 us (13%)
  local copies, waits for them, and re-layouts  52.5 us (8%)
  other arithmetic  39.7 us (6%)
    all_to_all x11, waiting for transfers between devices, sent_to_all(): return lax.all_to_all(copies, axis, split_axis=0, concat_axis=0, tiled=True)  109 us
    all_to_all x8, waiting for transfers between devices, sum_at_owner(): lax.all_to_all(split_up(shard, dim, length), axis, 0, 0, tiled=True)  82.5 us
    unnamed x1, blocking collectives  79.6 us
    dot_general x8, matrix products, section_block(): projected = jnp.dot(normed, w_in, preferred_element_type=jnp.float32)  54.2 us
    ppermute x8, waiting for transfers between devices, passed_along(): return lax.ppermute(block, axis, route)  53.8 us
    all_to_all x11, starting transfers between devices, sent_to_all(): return lax.all_to_all(copies, axis, split_axis=0, concat_axis=0, tiled=True)  42.8 us
    dot_general x8, matrix products, section_block(): partial_out = jnp.dot(mixed, out_proj, preferred_element_type=jnp.float32)  38.7 us
    all_gather x1, blocking collectives, shards(): lax.all_gather(query_tokens, ('dp', 'pipe'), axis=0, tiled=True)  34.2 us
  transfers between devices with their start and end apart: 29, of which 27 were waited for; matrix products, arithmetic and copies ran while one was open for 4% of the time, Pallas kernels for 0%

profile of v1, /device:TPU:0, one launch (start us, length us, event | category | flops | bytes accessed | tf_op | source)
XLA Modules:
  0.0 653.6 jit_solution(4935532351079515641)
XLA Ops:
  1.9 7.4 %all-to-all-start.2 = ((s32[32,2,32]{2,1,0:T(2,128)}), s32[32,2,32]{2,1,0:T(2,128)S(1)}, u32[]{:S(2)}, u32[]{:S(2)}) async-start(s32[32,2,32]{2,1,0:T(2,128)} %tile.2), calls=%async_computation.2 | async-start | bytes 65536 | tf_op jit(solution)/shard_map/all_to_all | solution.py:18
  9.4 34.2 %all-gather = s32[32,1,32]{2,1,0:T(1,128)S(1)} all-gather(s32[1,1,32]{2,1,0:T(1,128)} %bitcast.146), channel_id=1, replica_groups=mesh['dp'=8,'pipe'=4,'tensor'=4] {'dp','pipe'}, dimensions={0}, use_global_device_ids=true | all-gather | bytes 4224 | tf_op jit(solution)/shard_map/all_gather | solution.py:111
  43.9 18.7 %gather_fusion = bf16[3072,1024]{1,0:T(8,128)(2,1)} fusion(bf16[2004,1024]{1,0:T(8,128)(2,1)} %param.21, s32[3072]{0:T(1024)S(1)} %broadcast_clamp_fusion.1), kind=kCustom, calls=%fused_computation | custom fusion | bytes 12595200 | tf_op jit(solution)/shard_map/jit(_take)/gather | solution.py:120
  62.5 7.0 %select_select_fusion = bf16[32,96,1024]{2,1,0:T(8,128)(2,1)} fusion(bf16[32,96,1024]{2,1,0:T(8,128)(2,1)} %bitcast.127, pred[32,96]{1,0:T(8,128)(4,1)S(1)} %get-tuple-element.312, pred[32,96]{1,0:T(8,128)(4,1)S(1)} %get-tuple-element.322), kind=kLoop, calls=%fused_computation.56 | loop fusion | flops 6291456 | bytes 12589056 | tf_op jit(solution)/shard_map/jit(_where)/select_n | solution.py:121
  69.5 5.0 all-to-all-start.3
  77.5 79.6 %all-reduce.2 = (s32[64]{0:T(128)S(1)}, s32[32]{0:T(128)S(1)}) all-reduce(s32[64]{0:T(128)S(1)} %dynamic-update-slice, s32[32]{0:T(128)S(1)} %dynamic-update-slice.1), channel_id=1, replica_groups=mesh['dp'=8,'pipe'=4,'tensor'=4] {'dp','pipe'}, use_global_device_ids=true, to_apply=%add | all-reduce | flops 96 | bytes 768
  157.0 11.6 %pad_maximum_fusion = bf16[4096,1536]{1,0:T(8,128)(2,1)} fusion(bf16[4096,256]{1,0:T(8,128)(2,1)S(1)} %bitcast.134, bf16[4096,256]{1,0:T(8,128)(2,1)} %bitcast.135, bf16[4096,1024]{1,0:T(8,128)(2,1)} %bitcast.128), kind=kLoop, calls=%fused_computation.55 | loop fusion | flops 37748736 | bytes 25165824 | tf_op jit(solution)/shard_map/concatenate | solution.py:135
  172.9 409.0 %while.16 = (s32[]{:T(128)}, bf16[96,1024]{1,0:T(8,128)(2,1)S(1)}, s32[]{:T(128)}, f32[1,4096]{1,0:T(1,128)S(1)}, bf16[4096,1536]{1,0:T(8,128)(2,1)}, /*index=5*...) while((s32[]{:T(128)}, bf16[96,1024]{1,0:T(8,128)(2,1)S(1)}, ...), condition=%wide.region_6.7_spmd.clone, body=%wide.region_1.0_spmd.clone.sunk | while | flops 2038168704 | bytes 45535072 | solution.py:187
  174.0 5.3 all-to-all-start
  180.9 10.2 %all-to-all-done = bf16[4,96,1024]{2,1,0:T(8,128)(2,1)S(1)} async-done(((bf16[4,96,1024]{2,1,0:T(8,128)(2,1)}), bf16[4,96,1024]{2,1,0:T(8,128)(2,1)S(1)}, u32[]{:S(2)}, u32[]{:S(2)}) %all-to-all-start) | async-done | bytes 786464 | tf_op jit(solution)/shard_map/while/body/eval_jaxpr/all_to_all | solution.py:31
  191.7 6.8 %fusion.84 = f32[96,1536]{1,0:T(8,128)S(1)} fusion(bf16[4096,1536]{1,0:T(8,128)(2,1)} %get-tuple-element.430, f32[96,4096]{1,0:T(8,128)S(1)} %bitcast.124, f32[4096]{0:T(1024)S(1)} %bitcast.136, f32[96]{0:T(128)S(1)} %add_rsqrt_fusion.3), kind=kOutput, calls=%fused_computation.17.clone.1 | convolution fusion | flops 1209139200 | bytes 14762368 | tf_op jit(solution)/shard_map/while/body/eval_jaxpr/dot_general | solution.py:143
  200.7 4.8 convolution_convert_fusion.4
  210.1 11.0 %all-to-all-done.1 = bf16[4,96,1024]{2,1,0:T(8,128)(2,1)S(1)} async-done(((bf16[4,96,1024]{2,1,0:T(8,128)(2,1)}), bf16[4,96,1024]{2,1,0:T(8,128)(2,1)S(1)}, u32[]{:S(2)}, u32[]{:S(2)}) %all-to-all-start.1) | async-done | bytes 786464 | tf_op jit(solution)/shard_map/while/body/eval_jaxpr/all_to_all | solution.py:46
  222.4 5.8 collective-permute-done
  234.4 7.8 %all-to-all-done = bf16[4,96,1024]{2,1,0:T(8,128)(2,1)S(1)} async-done(((bf16[4,96,1024]{2,1,0:T(8,128)(2,1)}), bf16[4,96,1024]{2,1,0:T(8,128)(2,1)S(1)}, u32[]{:S(2)}, u32[]{:S(2)}) %all-to-all-start) | async-done | bytes 786464 | tf_op jit(solution)/shard_map/while/body/eval_jaxpr/all_to_all | solution.py:31
  242.7 6.8 %fusion.84 = f32[96,1536]{1,0:T(8,128)S(1)} fusion(bf16[4096,1536]{1,0:T(8,128)(2,1)} %get-tuple-element.430, f32[96,4096]{1,0:T(8,128)S(1)} %bitcast.124, f32[4096]{0:T(1024)S(1)} %bitcast.136, f32[96]{0:T(128)S(1)} %add_rsqrt_fusion.3), kind=kOutput, calls=%fused_computation.17.clone.1 | convolution fusion | flops 1209139200 | bytes 14762368 | tf_op jit(solution)/shard_map/while/body/eval_jaxpr/dot_general | solution.py:143
  251.8 4.8 convolution_convert_fusion.4
  261.1 9.4 %all-to-all-done.1 = bf16[4,96,1024]{2,1,0:T(8,128)(2,1)S(1)} async-done(((bf16[4,96,1024]{2,1,0:T(8,128)(2,1)}), bf16[4,96,1024]{2,1,0:T(8,128)(2,1)S(1)}, u32[]{:S(2)}, u32[]{:S(2)}) %all-to-all-start.1) | async-done | bytes 786464 | tf_op jit(solution)/shard_map/while/body/eval_jaxpr/all_to_all | solution.py:46
  270.8 6.9 %collective-permute-done = bf16[96,1024]{1,0:T(8,128)(2,1)S(1)} collective-permute-done((bf16[96,1024]{1,0:T(8,128)(2,1)S(1)}, bf16[96,1024]{1,0:T(8,128)(2,1)S(1)}, u32[]{:S(2)}, u32[]{:S(2)}) %collective-permute-start) | collective-permute-done | bytes 196640 | tf_op jit(solution)/shard_map/while/body/eval_jaxpr/ppermute | solution.py:53
  283.9 7.8 %all-to-all-done = bf16[4,96,1024]{2,1,0:T(8,128)(2,1)S(1)} async-done(((bf16[4,96,1024]{2,1,0:T(8,128)(2,1)}), bf16[4,96,1024]{2,1,0:T(8,128)(2,1)S(1)}, u32[]{:S(2)}, u32[]{:S(2)}) %all-to-all-start) | async-done | bytes 786464 | tf_op jit(solution)/shard_map/while/body/eval_jaxpr/all_to_all | solution.py:31
  292.2 6.8 %fusion.84 = f32[96,1536]{1,0:T(8,128)S(1)} fusion(bf16[4096,1536]{1,0:T(8,128)(2,1)} %get-tuple-element.430, f32[96,4096]{1,0:T(8,128)S(1)} %bitcast.124, f32[4096]{0:T(1024)S(1)} %bitcast.136, f32[96]{0:T(128)S(1)} %add_rsqrt_fusion.3), kind=kOutput, calls=%fused_computation.17.clone.1 | convolution fusion | flops 1209139200 | bytes 14762368 | tf_op jit(solution)/shard_map/while/body/eval_jaxpr/dot_general | solution.py:143
  310.6 9.4 %all-to-all-done.1 = bf16[4,96,1024]{2,1,0:T(8,128)(2,1)S(1)} async-done(((bf16[4,96,1024]{2,1,0:T(8,128)(2,1)}), bf16[4,96,1024]{2,1,0:T(8,128)(2,1)S(1)}, u32[]{:S(2)}, u32[]{:S(2)}) %all-to-all-start.1) | async-done | bytes 786464 | tf_op jit(solution)/shard_map/while/body/eval_jaxpr/all_to_all | solution.py:46
  320.3 6.9 %collective-permute-done = bf16[96,1024]{1,0:T(8,128)(2,1)S(1)} collective-permute-done((bf16[96,1024]{1,0:T(8,128)(2,1)S(1)}, bf16[96,1024]{1,0:T(8,128)(2,1)S(1)}, u32[]{:S(2)}, u32[]{:S(2)}) %collective-permute-start) | collective-permute-done | bytes 196640 | tf_op jit(solution)/shard_map/while/body/eval_jaxpr/ppermute | solution.py:53
  333.4 7.8 %all-to-all-done = bf16[4,96,1024]{2,1,0:T(8,128)(2,1)S(1)} async-done(((bf16[4,96,1024]{2,1,0:T(8,128)(2,1)}), bf16[4,96,1024]{2,1,0:T(8,128)(2,1)S(1)}, u32[]{:S(2)}, u32[]{:S(2)}) %all-to-all-start) | async-done | bytes 786464 | tf_op jit(solution)/shard_map/while/body/eval_jaxpr/all_to_all | solution.py:31
  341.7 6.8 %fusion.84 = f32[96,1536]{1,0:T(8,128)S(1)} fusion(bf16[4096,1536]{1,0:T(8,128)(2,1)} %get-tuple-element.430, f32[96,4096]{1,0:T(8,128)S(1)} %bitcast.124, f32[4096]{0:T(1024)S(1)} %bitcast.136, f32[96]{0:T(128)S(1)} %add_rsqrt_fusion.3), kind=kOutput, calls=%fused_computation.17.clone.1 | convolution fusion | flops 1209139200 | bytes 14762368 | tf_op jit(solution)/shard_map/while/body/eval_jaxpr/dot_general | solution.py:143
  360.1 9.4 %all-to-all-done.1 = bf16[4,96,1024]{2,1,0:T(8,128)(2,1)S(1)} async-done(((bf16[4,96,1024]{2,1,0:T(8,128)(2,1)}), bf16[4,96,1024]{2,1,0:T(8,128)(2,1)S(1)}, u32[]{:S(2)}, u32[]{:S(2)}) %all-to-all-start.1) | async-done | bytes 786464 | tf_op jit(solution)/shard_map/while/body/eval_jaxpr/all_to_all | solution.py:46
  369.8 6.9 %collective-permute-done = bf16[96,1024]{1,0:T(8,128)(2,1)S(1)} collective-permute-done((bf16[96,1024]{1,0:T(8,128)(2,1)S(1)}, bf16[96,1024]{1,0:T(8,128)(2,1)S(1)}, u32[]{:S(2)}, u32[]{:S(2)}) %collective-permute-start) | collective-permute-done | bytes 196640 | tf_op jit(solution)/shard_map/while/body/eval_jaxpr/ppermute | solution.py:53
  382.9 7.8 %all-to-all-done = bf16[4,96,1024]{2,1,0:T(8,128)(2,1)S(1)} async-done(((bf16[4,96,1024]{2,1,0:T(8,128)(2,1)}), bf16[4,96,1024]{2,1,0:T(8,128)(2,1)S(1)}, u32[]{:S(2)}, u32[]{:S(2)}) %all-to-all-start) | async-done | bytes 786464 | tf_op jit(solution)/shard_map/while/body/eval_jaxpr/all_to_all | solution.py:31
  391.2 6.8 %fusion.84 = f32[96,1536]{1,0:T(8,128)S(1)} fusion(bf16[4096,1536]{1,0:T(8,128)(2,1)} %get-tuple-element.430, f32[96,4096]{1,0:T(8,128)S(1)} %bitcast.124, f32[4096]{0:T(1024)S(1)} %bitcast.136, f32[96]{0:T(128)S(1)} %add_rsqrt_fusion.3), kind=kOutput, calls=%fused_computation.17.clone.1 | convolution fusion | flops 1209139200 | bytes 14762368 | tf_op jit(solution)/shard_map/while/body/eval_jaxpr/dot_general | solution.py:143
  409.6 10.7 %all-to-all-done.1 = bf16[4,96,1024]{2,1,0:T(8,128)(2,1)S(1)} async-done(((bf16[4,96,1024]{2,1,0:T(8,128)(2,1)}), bf16[4,96,1024]{2,1,0:T(8,128)(2,1)S(1)}, u32[]{:S(2)}, u32[]{:S(2)}) %all-to-all-start.1) | async-done | bytes 786464 | tf_op jit(solution)/shard_map/while/body/eval_jaxpr/all_to_all | solution.py:46
  420.6 6.9 %collective-permute-done = bf16[96,1024]{1,0:T(8,128)(2,1)S(1)} collective-permute-done((bf16[96,1024]{1,0:T(8,128)(2,1)S(1)}, bf16[96,1024]{1,0:T(8,128)(2,1)S(1)}, u32[]{:S(2)}, u32[]{:S(2)}) %collective-permute-start) | collective-permute-done | bytes 196640 | tf_op jit(solution)/shard_map/while/body/eval_jaxpr/ppermute | solution.py:53
  433.7 7.8 %all-to-all-done = bf16[4,96,1024]{2,1,0:T(8,128)(2,1)S(1)} async-done(((bf16[4,96,1024]{2,1,0:T(8,128)(2,1)}), bf16[4,96,1024]{2,1,0:T(8,128)(2,1)S(1)}, u32[]{:S(2)}, u32[]{:S(2)}) %all-to-all-start) | async-done | bytes 786464 | tf_op jit(solution)/shard_map/while/body/eval_jaxpr/all_to_all | solution.py:31
  442.0 6.8 %fusion.84 = f32[96,1536]{1,0:T(8,128)S(1)} fusion(bf16[4096,1536]{1,0:T(8,128)(2,1)} %get-tuple-element.430, f32[96,4096]{1,0:T(8,128)S(1)} %bitcast.124, f32[4096]{0:T(1024)S(1)} %bitcast.136, f32[96]{0:T(128)S(1)} %add_rsqrt_fusion.3), kind=kOutput, calls=%fused_computation.17.clone.1 | convolution fusion | flops 1209139200 | bytes 14762368 | tf_op jit(solution)/shard_map/while/body/eval_jaxpr/dot_general | solution.py:143
  460.4 13.1 %all-to-all-done.1 = bf16[4,96,1024]{2,1,0:T(8,128)(2,1)S(1)} async-done(((bf16[4,96,1024]{2,1,0:T(8,128)(2,1)}), bf16[4,96,1024]{2,1,0:T(8,128)(2,1)S(1)}, u32[]{:S(2)}, u32[]{:S(2)}) %all-to-all-start.1) | async-done | bytes 786464 | tf_op jit(solution)/shard_map/while/body/eval_jaxpr/all_to_all | solution.py:46
  473.8 6.9 %collective-permute-done = bf16[96,1024]{1,0:T(8,128)(2,1)S(1)} collective-permute-done((bf16[96,1024]{1,0:T(8,128)(2,1)S(1)}, bf16[96,1024]{1,0:T(8,128)(2,1)S(1)}, u32[]{:S(2)}, u32[]{:S(2)}) %collective-permute-start) | collective-permute-done | bytes 196640 | tf_op jit(solution)/shard_map/while/body/eval_jaxpr/ppermute | solution.py:53
  486.8 7.8 %all-to-all-done = bf16[4,96,1024]{2,1,0:T(8,128)(2,1)S(1)} async-done(((bf16[4,96,1024]{2,1,0:T(8,128)(2,1)}), bf16[4,96,1024]{2,1,0:T(8,128)(2,1)S(1)}, u32[]{:S(2)}, u32[]{:S(2)}) %all-to-all-start) | async-done | bytes 786464 | tf_op jit(solution)/shard_map/while/body/eval_jaxpr/all_to_all | solution.py:31
  495.1 6.8 %fusion.84 = f32[96,1536]{1,0:T(8,128)S(1)} fusion(bf16[4096,1536]{1,0:T(8,128)(2,1)} %get-tuple-element.430, f32[96,4096]{1,0:T(8,128)S(1)} %bitcast.124, f32[4096]{0:T(1024)S(1)} %bitcast.136, f32[96]{0:T(128)S(1)} %add_rsqrt_fusion.3), kind=kOutput, calls=%fused_computation.17.clone.1 | convolution fusion | flops 1209139200 | bytes 14762368 | tf_op jit(solution)/shard_map/while/body/eval_jaxpr/dot_general | solution.py:143
  513.5 10.0 %all-to-all-done.1 = bf16[4,96,1024]{2,1,0:T(8,128)(2,1)S(1)} async-done(((bf16[4,96,1024]{2,1,0:T(8,128)(2,1)}), bf16[4,96,1024]{2,1,0:T(8,128)(2,1)S(1)}, u32[]{:S(2)}, u32[]{:S(2)}) %all-to-all-start.1) | async-done | bytes 786464 | tf_op jit(solution)/shard_map/while/body/eval_jaxpr/all_to_all | solution.py:46
  523.8 6.9 %collective-permute-done = bf16[96,1024]{1,0:T(8,128)(2,1)S(1)} collective-permute-done((bf16[96,1024]{1,0:T(8,128)(2,1)S(1)}, bf16[96,1024]{1,0:T(8,128)(2,1)S(1)}, u32[]{:S(2)}, u32[]{:S(2)}) %collective-permute-start) | collective-permute-done | bytes 196640 | tf_op jit(solution)/shard_map/while/body/eval_jaxpr/ppermute | solution.py:53
  536.8 9.6 %all-to-all-done = bf16[4,96,1024]{2,1,0:T(8,128)(2,1)S(1)} async-done(((bf16[4,96,1024]{2,1,0:T(8,128)(2,1)}), bf16[4,96,1024]{2,1,0:T(8,128)(2,1)S(1)}, u32[]{:S(2)}, u32[]{:S(2)}) %all-to-all-start) | async-done | bytes 786464 | tf_op jit(solution)/shard_map/while/body/eval_jaxpr/all_to_all | solution.py:31
  547.0 6.8 %fusion.84 = f32[96,1536]{1,0:T(8,128)S(1)} fusion(bf16[4096,1536]{1,0:T(8,128)(2,1)} %get-tuple-element.430, f32[96,4096]{1,0:T(8,128)S(1)} %bitcast.124, f32[4096]{0:T(1024)S(1)} %bitcast.136, f32[96]{0:T(128)S(1)} %add_rsqrt_fusion.3), kind=kOutput, calls=%fused_computation.17.clone.1 | convolution fusion | flops 1209139200 | bytes 14762368 | tf_op jit(solution)/shard_map/while/body/eval_jaxpr/dot_general | solution.py:143
  565.3 9.4 %all-to-all-done.1 = bf16[4,96,1024]{2,1,0:T(8,128)(2,1)S(1)} async-done(((bf16[4,96,1024]{2,1,0:T(8,128)(2,1)}), bf16[4,96,1024]{2,1,0:T(8,128)(2,1)S(1)}, u32[]{:S(2)}, u32[]{:S(2)}) %all-to-all-start.1) | async-done | bytes 786464 | tf_op jit(solution)/shard_map/while/body/eval_jaxpr/all_to_all | solution.py:46
  575.0 6.9 %collective-permute-done = bf16[96,1024]{1,0:T(8,128)(2,1)S(1)} collective-permute-done((bf16[96,1024]{1,0:T(8,128)(2,1)S(1)}, bf16[96,1024]{1,0:T(8,128)(2,1)S(1)}, u32[]{:S(2)}, u32[]{:S(2)}) %collective-permute-start) | collective-permute-done | bytes 196640 | tf_op jit(solution)/shard_map/while/body/eval_jaxpr/ppermute | solution.py:53
  586.6 9.2 %all-to-all-done.4 = bf16[4,96,1024]{2,1,0:T(8,128)(2,1)S(1)} async-done(((bf16[4,96,1024]{2,1,0:T(8,128)(2,1)}), bf16[4,96,1024]{2,1,0:T(8,128)(2,1)S(1)}, u32[]{:S(2)}, u32[]{:S(2)}) %all-to-all-start.4) | async-done | bytes 786464 | tf_op jit(solution)/shard_map/all_to_all | solution.py:31
  596.5 5.5 all-to-all-start.6
  603.3 6.0 all-to-all-done.6
  615.6 27.6 %all-to-all-done.5 = bf16[32,32,1024]{2,1,0:T(8,128)(2,1)S(1)} async-done(((bf16[32,32,1024]{2,1,0:T(8,128)(2,1)}), bf16[32,32,1024]{2,1,0:T(8,128)(2,1)S(1)}, u32[]{:S(2)}, u32[]{:S(2)}) %all-to-all-start.5) | async-done | bytes 2097184 | tf_op jit(solution)/shard_map/all_to_all | solution.py:31
  644.2 8.9 %psum.7 = f32[1,16]{1,0:T(1,128)S(1)} all-reduce(f32[1,16]{1,0:T(1,128)S(1)} %bitcast.145), channel_id=1, replica_groups=mesh['dp'=8,'pipe'=4,'tensor'=4] {'tensor'}, use_global_device_ids=true, to_apply=%region_13.14 | all-reduce | flops 16 | bytes 128 | tf_op jit(solution)/shard_map/psum | solution.py:216
  (328 shorter events, 156.7 us)
Async XLA Ops:
  1.9 41.6 %all-to-all-start.2 = ((s32[32,2,32]{2,1,0:T(2,128)}), s32[32,2,32]{2,1,0:T(2,128)S(1)}, u32[]{:S(2)}, u32[]{:S(2)}) async-start(s32[32,2,32]{2,1,0:T(2,128)} %tile.2), calls=%async_computation.2 | async-start | bytes 65536 | tf_op jit(solution)/shard_map/all_to_all | solution.py:18
  69.5 5.7 copy-start.5
  69.5 7.0 %copy-start.4 = (s32[2]{0:T(128)S(1)}, s32[2]{0:T(128)}, u32[]{:S(2)}) copy-start(s32[2]{0:T(128)} %param.16) | copy-start | bytes 28
  69.5 87.5 %copy-start = (bf16[1,4096,256]{2,1,0:T(8,128)(2,1)S(1)}, bf16[1,4096,256]{2,1,0:T(8,128)(2,1)}, u32[]{:S(2)}) copy-start(bf16[1,4096,256]{2,1,0:T(8,128)(2,1)} %param.25) | copy-start | bytes 6291460
  69.5 99.1 %all-to-all-start.3 = ((bf16[32,96,1024]{2,1,0:T(8,128)(2,1)}), bf16[32,96,1024]{2,1,0:T(8,128)(2,1)}, u32[]{:S(2)}, u32[]{:S(2)}) async-start(bf16[32,96,1024]{2,1,0:T(8,128)(2,1)} %select_select_fusion), calls=%async_computation.3 | async-start | bytes 12582912 | tf_op jit(solution)/shard_map/all_to_all | solution.py:122
  168.6 4.3 copy-start.1
  172.9 413.6 %copy-start.3 = (s32[2,1]{0,1:T(1,128)S(1)}, s32[2,1]{0,1:T(1,128)}, u32[]{:S(2)}) copy-start(s32[2,1]{0,1:T(1,128)} %param.17) | copy-start | bytes 28
  174.0 17.2 %all-to-all-start = ((bf16[4,96,1024]{2,1,0:T(8,128)(2,1)}), bf16[4,96,1024]{2,1,0:T(8,128)(2,1)S(1)}, u32[]{:S(2)}, u32[]{:S(2)}) async-start(bf16[4,96,1024]{2,1,0:T(8,128)(2,1)} %broadcast_in_dim.169), calls=%async_computation | async-start | bytes 1572864 | tf_op jit(solution)/shard_map/while/body/eval_jaxpr/all_to_all | solution.py:31
  206.6 14.5 %all-to-all-start.1 = ((bf16[4,96,1024]{2,1,0:T(8,128)(2,1)}), bf16[4,96,1024]{2,1,0:T(8,128)(2,1)S(1)}, u32[]{:S(2)}, u32[]{:S(2)}) async-start(bf16[4,96,1024]{2,1,0:T(8,128)(2,1)} %bitcast.121), calls=%async_computation.1 | async-start | bytes 1572864 | tf_op jit(solution)/shard_map/while/body/eval_jaxpr/all_to_all | solution.py:46
  221.2 6.9 %collective-permute-start = (bf16[96,1024]{1,0:T(8,128)(2,1)S(1)}, bf16[96,1024]{1,0:T(8,128)(2,1)S(1)}, u32[]{:S(2)}, u32[]{:S(2)}) collective-permute-start(bf16[96,1024]{1,0:T(8,128)(2,1)S(1)} %fusion.89), channel_id=1, source_target_pairs={{12,0},{0,4},{4,8},{8,12},{13,1},{1,5},{5,9},{9,13},{14,2},{2,6},{... | collective-permute-start | bytes 589832 | tf_op jit(solution)/shard_map/while/body/eval_jaxpr/ppermute | solution.py:53
  229.2 13.0 %all-to-all-start = ((bf16[4,96,1024]{2,1,0:T(8,128)(2,1)}), bf16[4,96,1024]{2,1,0:T(8,128)(2,1)S(1)}, u32[]{:S(2)}, u32[]{:S(2)}) async-start(bf16[4,96,1024]{2,1,0:T(8,128)(2,1)} %broadcast_in_dim.169), calls=%async_computation | async-start | bytes 1572864 | tf_op jit(solution)/shard_map/while/body/eval_jaxpr/all_to_all | solution.py:31
  257.6 13.0 %all-to-all-start.1 = ((bf16[4,96,1024]{2,1,0:T(8,128)(2,1)}), bf16[4,96,1024]{2,1,0:T(8,128)(2,1)S(1)}, u32[]{:S(2)}, u32[]{:S(2)}) async-start(bf16[4,96,1024]{2,1,0:T(8,128)(2,1)} %bitcast.121), calls=%async_computation.1 | async-start | bytes 1572864 | tf_op jit(solution)/shard_map/while/body/eval_jaxpr/all_to_all | solution.py:46
  270.7 6.9 %collective-permute-start = (bf16[96,1024]{1,0:T(8,128)(2,1)S(1)}, bf16[96,1024]{1,0:T(8,128)(2,1)S(1)}, u32[]{:S(2)}, u32[]{:S(2)}) collective-permute-start(bf16[96,1024]{1,0:T(8,128)(2,1)S(1)} %fusion.89), channel_id=1, source_target_pairs={{12,0},{0,4},{4,8},{8,12},{13,1},{1,5},{5,9},{9,13},{14,2},{2,6},{... | collective-permute-start | bytes 589832 | tf_op jit(solution)/shard_map/while/body/eval_jaxpr/ppermute | solution.py:53
  278.7 13.0 %all-to-all-start = ((bf16[4,96,1024]{2,1,0:T(8,128)(2,1)}), bf16[4,96,1024]{2,1,0:T(8,128)(2,1)S(1)}, u32[]{:S(2)}, u32[]{:S(2)}) async-start(bf16[4,96,1024]{2,1,0:T(8,128)(2,1)} %broadcast_in_dim.169), calls=%async_computation | async-start | bytes 1572864 | tf_op jit(solution)/shard_map/while/body/eval_jaxpr/all_to_all | solution.py:31
  307.1 13.0 %all-to-all-start.1 = ((bf16[4,96,1024]{2,1,0:T(8,128)(2,1)}), bf16[4,96,1024]{2,1,0:T(8,128)(2,1)S(1)}, u32[]{:S(2)}, u32[]{:S(2)}) async-start(bf16[4,96,1024]{2,1,0:T(8,128)(2,1)} %bitcast.121), calls=%async_computation.1 | async-start | bytes 1572864 | tf_op jit(solution)/shard_map/while/body/eval_jaxpr/all_to_all | solution.py:46
  320.2 6.9 %collective-permute-start = (bf16[96,1024]{1,0:T(8,128)(2,1)S(1)}, bf16[96,1024]{1,0:T(8,128)(2,1)S(1)}, u32[]{:S(2)}, u32[]{:S(2)}) collective-permute-start(bf16[96,1024]{1,0:T(8,128)(2,1)S(1)} %fusion.89), channel_id=1, source_target_pairs={{12,0},{0,4},{4,8},{8,12},{13,1},{1,5},{5,9},{9,13},{14,2},{2,6},{... | collective-permute-start | bytes 589832 | tf_op jit(solution)/shard_map/while/body/eval_jaxpr/ppermute | solution.py:53
  328.2 13.0 %all-to-all-start = ((bf16[4,96,1024]{2,1,0:T(8,128)(2,1)}), bf16[4,96,1024]{2,1,0:T(8,128)(2,1)S(1)}, u32[]{:S(2)}, u32[]{:S(2)}) async-start(bf16[4,96,1024]{2,1,0:T(8,128)(2,1)} %broadcast_in_dim.169), calls=%async_computation | async-start | bytes 1572864 | tf_op jit(solution)/shard_map/while/body/eval_jaxpr/all_to_all | solution.py:31
  356.6 13.0 %all-to-all-start.1 = ((bf16[4,96,1024]{2,1,0:T(8,128)(2,1)}), bf16[4,96,1024]{2,1,0:T(8,128)(2,1)S(1)}, u32[]{:S(2)}, u32[]{:S(2)}) async-start(bf16[4,96,1024]{2,1,0:T(8,128)(2,1)} %bitcast.121), calls=%async_computation.1 | async-start | bytes 1572864 | tf_op jit(solution)/shard_map/while/body/eval_jaxpr/all_to_all | solution.py:46
  369.7 6.9 %collective-permute-start = (bf16[96,1024]{1,0:T(8,128)(2,1)S(1)}, bf16[96,1024]{1,0:T(8,128)(2,1)S(1)}, u32[]{:S(2)}, u32[]{:S(2)}) collective-permute-start(bf16[96,1024]{1,0:T(8,128)(2,1)S(1)} %fusion.89), channel_id=1, source_target_pairs={{12,0},{0,4},{4,8},{8,12},{13,1},{1,5},{5,9},{9,13},{14,2},{2,6},{... | collective-permute-start | bytes 589832 | tf_op jit(solution)/shard_map/while/body/eval_jaxpr/ppermute | solution.py:53
  377.7 13.0 %all-to-all-start = ((bf16[4,96,1024]{2,1,0:T(8,128)(2,1)}), bf16[4,96,1024]{2,1,0:T(8,128)(2,1)S(1)}, u32[]{:S(2)}, u32[]{:S(2)}) async-start(bf16[4,96,1024]{2,1,0:T(8,128)(2,1)} %broadcast_in_dim.169), calls=%async_computation | async-start | bytes 1572864 | tf_op jit(solution)/shard_map/while/body/eval_jaxpr/all_to_all | solution.py:31
  406.1 14.2 %all-to-all-start.1 = ((bf16[4,96,1024]{2,1,0:T(8,128)(2,1)}), bf16[4,96,1024]{2,1,0:T(8,128)(2,1)S(1)}, u32[]{:S(2)}, u32[]{:S(2)}) async-start(bf16[4,96,1024]{2,1,0:T(8,128)(2,1)} %bitcast.121), calls=%async_computation.1 | async-start | bytes 1572864 | tf_op jit(solution)/shard_map/while/body/eval_jaxpr/all_to_all | solution.py:46
  420.5 6.9 %collective-permute-start = (bf16[96,1024]{1,0:T(8,128)(2,1)S(1)}, bf16[96,1024]{1,0:T(8,128)(2,1)S(1)}, u32[]{:S(2)}, u32[]{:S(2)}) collective-permute-start(bf16[96,1024]{1,0:T(8,128)(2,1)S(1)} %fusion.89), channel_id=1, source_target_pairs={{12,0},{0,4},{4,8},{8,12},{13,1},{1,5},{5,9},{9,13},{14,2},{2,6},{... | collective-permute-start | bytes 589832 | tf_op jit(solution)/shard_map/while/body/eval_jaxpr/ppermute | solution.py:53
  428.5 13.0 %all-to-all-start = ((bf16[4,96,1024]{2,1,0:T(8,128)(2,1)}), bf16[4,96,1024]{2,1,0:T(8,128)(2,1)S(1)}, u32[]{:S(2)}, u32[]{:S(2)}) async-start(bf16[4,96,1024]{2,1,0:T(8,128)(2,1)} %broadcast_in_dim.169), calls=%async_computation | async-start | bytes 1572864 | tf_op jit(solution)/shard_map/while/body/eval_jaxpr/all_to_all | solution.py:31
  456.8 16.6 %all-to-all-start.1 = ((bf16[4,96,1024]{2,1,0:T(8,128)(2,1)}), bf16[4,96,1024]{2,1,0:T(8,128)(2,1)S(1)}, u32[]{:S(2)}, u32[]{:S(2)}) async-start(bf16[4,96,1024]{2,1,0:T(8,128)(2,1)} %bitcast.121), calls=%async_computation.1 | async-start | bytes 1572864 | tf_op jit(solution)/shard_map/while/body/eval_jaxpr/all_to_all | solution.py:46
  473.7 6.9 %collective-permute-start = (bf16[96,1024]{1,0:T(8,128)(2,1)S(1)}, bf16[96,1024]{1,0:T(8,128)(2,1)S(1)}, u32[]{:S(2)}, u32[]{:S(2)}) collective-permute-start(bf16[96,1024]{1,0:T(8,128)(2,1)S(1)} %fusion.89), channel_id=1, source_target_pairs={{12,0},{0,4},{4,8},{8,12},{13,1},{1,5},{5,9},{9,13},{14,2},{2,6},{... | collective-permute-start | bytes 589832 | tf_op jit(solution)/shard_map/while/body/eval_jaxpr/ppermute | solution.py:53
  481.6 13.0 %all-to-all-start = ((bf16[4,96,1024]{2,1,0:T(8,128)(2,1)}), bf16[4,96,1024]{2,1,0:T(8,128)(2,1)S(1)}, u32[]{:S(2)}, u32[]{:S(2)}) async-start(bf16[4,96,1024]{2,1,0:T(8,128)(2,1)} %broadcast_in_dim.169), calls=%async_computation | async-start | bytes 1572864 | tf_op jit(solution)/shard_map/while/body/eval_jaxpr/all_to_all | solution.py:31
  510.0 13.5 %all-to-all-start.1 = ((bf16[4,96,1024]{2,1,0:T(8,128)(2,1)}), bf16[4,96,1024]{2,1,0:T(8,128)(2,1)S(1)}, u32[]{:S(2)}, u32[]{:S(2)}) async-start(bf16[4,96,1024]{2,1,0:T(8,128)(2,1)} %bitcast.121), calls=%async_computation.1 | async-start | bytes 1572864 | tf_op jit(solution)/shard_map/while/body/eval_jaxpr/all_to_all | solution.py:46
  523.7 6.9 %collective-permute-start = (bf16[96,1024]{1,0:T(8,128)(2,1)S(1)}, bf16[96,1024]{1,0:T(8,128)(2,1)S(1)}, u32[]{:S(2)}, u32[]{:S(2)}) collective-permute-start(bf16[96,1024]{1,0:T(8,128)(2,1)S(1)} %fusion.89), channel_id=1, source_target_pairs={{12,0},{0,4},{4,8},{8,12},{13,1},{1,5},{5,9},{9,13},{14,2},{2,6},{... | collective-permute-start | bytes 589832 | tf_op jit(solution)/shard_map/while/body/eval_jaxpr/ppermute | solution.py:53
  531.7 14.7 %all-to-all-start = ((bf16[4,96,1024]{2,1,0:T(8,128)(2,1)}), bf16[4,96,1024]{2,1,0:T(8,128)(2,1)S(1)}, u32[]{:S(2)}, u32[]{:S(2)}) async-start(bf16[4,96,1024]{2,1,0:T(8,128)(2,1)} %broadcast_in_dim.169), calls=%async_computation | async-start | bytes 1572864 | tf_op jit(solution)/shard_map/while/body/eval_jaxpr/all_to_all | solution.py:31
  561.8 13.0 %all-to-all-start.1 = ((bf16[4,96,1024]{2,1,0:T(8,128)(2,1)}), bf16[4,96,1024]{2,1,0:T(8,128)(2,1)S(1)}, u32[]{:S(2)}, u32[]{:S(2)}) async-start(bf16[4,96,1024]{2,1,0:T(8,128)(2,1)} %bitcast.121), calls=%async_computation.1 | async-start | bytes 1572864 | tf_op jit(solution)/shard_map/while/body/eval_jaxpr/all_to_all | solution.py:46
  575.0 6.9 %collective-permute-start = (bf16[96,1024]{1,0:T(8,128)(2,1)S(1)}, bf16[96,1024]{1,0:T(8,128)(2,1)S(1)}, u32[]{:S(2)}, u32[]{:S(2)}) collective-permute-start(bf16[96,1024]{1,0:T(8,128)(2,1)S(1)} %fusion.89), channel_id=1, source_target_pairs={{12,0},{0,4},{4,8},{8,12},{13,1},{1,5},{5,9},{9,13},{14,2},{2,6},{... | collective-permute-start | bytes 589832 | tf_op jit(solution)/shard_map/while/body/eval_jaxpr/ppermute | solution.py:53
  582.9 13.0 %all-to-all-start.4 = ((bf16[4,96,1024]{2,1,0:T(8,128)(2,1)}), bf16[4,96,1024]{2,1,0:T(8,128)(2,1)S(1)}, u32[]{:S(2)}, u32[]{:S(2)}) async-start(bf16[4,96,1024]{2,1,0:T(8,128)(2,1)} %broadcast_in_dim.128), calls=%async_computation.4 | async-start | bytes 1572864 | tf_op jit(solution)/shard_map/all_to_all | solution.py:31
  586.4 16.2 %dynamic-slice-start = ((f32[4096]{0:T(1024)}, s32[]{:T(128)}), f32[1024]{0:T(1024)S(1)}, s32[]{:S(2)}) async-start(f32[4096]{0:T(1024)} %param.27, s32[]{:T(128)} %select_n.118), calls=%async_computation.7 | async-start | bytes 8704 | tf_op jit(solution)/shard_map/dynamic_slice | solution.py:188
  596.5 12.8 %all-to-all-start.6 = ((bf16[32,1,32]{2,1,0:T(2,128)(2,1)}), bf16[32,1,32]{2,1,0:T(2,128)(2,1)S(1)}, u32[]{:S(2)}, u32[]{:S(2)}) async-start(bf16[32,1,32]{2,1,0:T(2,128)(2,1)} %broadcast_in_dim.130), calls=%async_computation.6 | async-start | bytes 32768 | tf_op jit(solution)/shard_map/all_to_all | solution.py:31
  610.9 32.3 %all-to-all-start.5 = ((bf16[32,32,1024]{2,1,0:T(8,128)(2,1)}), bf16[32,32,1024]{2,1,0:T(8,128)(2,1)S(1)}, u32[]{:S(2)}, u32[]{:S(2)}) async-start(bf16[32,32,1024]{2,1,0:T(8,128)(2,1)} %broadcast_in_dim.129), calls=%async_computation.5 | async-start | bytes 4194304 | tf_op jit(solution)/shard_map/all_to_all | solution.py:31
  643.7 10.0 %copy-start.2 = (f32[32,1024]{1,0:T(8,128)}, f32[32,1024]{1,0:T(8,128)S(1)}, u32[]{:S(2)}) copy-start(f32[32,1024]{1,0:T(8,128)S(1)} %broadcast_divide_fusion) | copy-start | bytes 393220
